TPU v7x, 256 devices: a whole 4x4x8 slice. The times are simulated.
256 devices in a mesh: scen: 16 (over z, y_hi), gen: 16 (over y_lo, x, core).
Axes of the slice: x: 4, y: 4 (y_hi: 2, y_lo: 2; y = y_hi * 2 + y_lo), z: 8, core: 2. Of those that a mesh axis runs over, the one named last changes fastest.
Arguments:
- zone_load: float32 [256, 16, 256], P('scen'), may hold values from 0.3 to 1
- linear_cost: float32 [16, 20480], P(None, 'gen'), may hold values from -4 to 4
- cost_diag: float32 [20480], P('gen'), may hold values from 0.5 to 2
- capacity: float32 [20480], P('gen'), may hold values from 0.5 to 2
- cost_tiles: bfloat16 [80, 256, 256], P('gen'), may hold values from -0.375 to 0.375
- coupling_tiles: bfloat16 [16, 80, 256, 256], P('scen', 'gen'), may hold values from -0.375 to 0.375
- block_map: int32 [16, 80], P('scen', 'gen'), may hold values 0 or 1
- zone_index: int32 [20480], P('gen'), may hold values from 0 to 255
- step_numer: int32 [5], replicated, may hold values from 1 to 4
- step_denom: int32 [5], replicated, may hold values from 5 to 8
Outputs:
- dispatch: float32 [256, 16, 20480], P('scen', None, 'gen')
- prices: float32 [256, 16, 256], P('scen')
- plan: float32 [16, 20480], P(None, 'gen')
All inputs are finite; a program needn't handle non-finite values. No bound on the sum of `block_map` on one device may be relied on, other than what follows from the above.
Results may differ from a plain program's by a relative error of at most 0.0003.
Values sent between devices are 32-bit elements; how exact they have to be, the bound alone decides.
A program may use at most 64 MiB of HBM per device.

v0:
```python
import jax
import jax.numpy as jnp
from jax import lax
from jax.sharding import Mesh
from jax.sharding import PartitionSpec as P

G = 20480
ITERS = 5
GEN = ("gen_0", "gen_1", "gen_2")
SCEN = ("scen_0", "scen_1")
SCEN_GEN = ("scen_0", "scen_1", "gen_0", "gen_1", "gen_2")
penalty = 2.0
centering = 0.5
epsilon = 1e-06


def copy_for_each(value, axis):
    copies = jnp.broadcast_to(value, (lax.axis_size(axis), *value.shape))
    return lax.all_to_all(copies, axis, split_axis=0, concat_axis=0, tiled=True)


def taken_together(value, axis):
    return copy_for_each(value, axis).sum(axis=0)


def over_pieces(value, axis):
    blocks = lax.all_gather(value, axis)
    return blocks.sum(axis=0)


def by_axis(value, axes):
    for axis in axes:
        value = lax.psum(value, axis)
    return value


def local(
    zone_load,
    linear_cost,
    cost_diag,
    capacity,
    cost_tiles,
    coupling_tiles,
    block_map,
    zone_index,
    step_numer,
    step_denom,
):
    local_scen = zone_load.shape[0]
    periods = linear_cost.shape[0]
    zone_count = zone_load.shape[2]
    local_gen = capacity.shape[0]
    local_blocks = cost_tiles.shape[0]
    tile_width = cost_tiles.shape[2]
    gen_devices = lax.axis_size(GEN)
    total_scen = local_scen * lax.axis_size(SCEN)
    row_count = local_scen * periods
    entries = float(total_scen * periods * G)
    coupling = coupling_tiles[0]
    block_mask = block_map[0].astype(jnp.float32)
    onehot = (zone_index[:, None] == jnp.arange(zone_count, dtype=jnp.int32)[None, :]).astype(
        jnp.float32
    )
    scen_ids = lax.axis_index(SCEN) * local_scen + jnp.arange(local_scen, dtype=jnp.int32)
    levels = 0.2 + 0.6 * (scen_ids.astype(jnp.float32) + 0.5) / total_scen
    dispatch = jnp.broadcast_to(levels[:, None, None] * capacity, (local_scen, periods, local_gen))
    low_dual = jnp.ones((local_scen, periods, local_gen), jnp.float32)
    high_dual = jnp.ones((local_scen, periods, local_gen), jnp.float32)
    prices = jnp.zeros((local_scen, periods, zone_count), jnp.float32)
    lowest = 0.02 * capacity
    highest = 0.98 * capacity
    plan = jnp.zeros((periods, local_gen), jnp.float32)
    for iteration in range(ITERS):
        step_size = step_numer[iteration].astype(jnp.float32) / step_denom[iteration].astype(
            jnp.float32
        )
        column_sums = taken_together(jnp.sum(dispatch, axis=0), SCEN)
        plan = column_sums / total_scen
        partial_value = jnp.dot(
            dispatch.reshape(row_count, local_gen),
            onehot,
            precision=lax.Precision.HIGHEST,
            preferred_element_type=jnp.float32,
        )
        totals = over_pieces(partial_value, GEN)
        imbalance = totals.reshape(local_scen, periods, zone_count) * (zone_count / G) - zone_load
        primal_local = jnp.sum(imbalance * imbalance) / gen_devices
        rounded = dispatch.astype(jnp.bfloat16).reshape(row_count, local_blocks, tile_width)
        cross_part = jnp.einsum(
            "rki,kij->rkj", rounded, coupling, preferred_element_type=jnp.float32
        )
        own_part = jnp.einsum(
            "rki,kij->rkj", rounded, cost_tiles, preferred_element_type=jnp.float32
        )
        products = (own_part + cross_part * block_mask[None, :, None]).reshape(
            local_scen, periods, local_gen
        )
        price_terms = jnp.dot(
            prices.reshape(row_count, zone_count),
            onehot.T,
            precision=lax.Precision.HIGHEST,
            preferred_element_type=jnp.float32,
        )
        residual = (
            cost_diag * dispatch
            + products
            + linear_cost
            + penalty * (dispatch - plan)
            + price_terms.reshape(local_scen, periods, local_gen)
            - low_dual
            + high_dual
        )
        gap_local = jnp.sum(dispatch * low_dual + (capacity - dispatch) * high_dual)
        dual_local = jnp.sum(residual * residual)
        stacked = jnp.stack([gap_local, dual_local, primal_local])
        summed = by_axis(stacked, SCEN_GEN)
        gap_sum = summed[0]
        dual_sq = summed[1]
        primal_sq = summed[2]
        target = centering * gap_sum / (2.0 * entries)
        dual_rms = jnp.sqrt(dual_sq / entries + epsilon)
        primal_rms = jnp.sqrt(primal_sq / float(total_scen * periods * zone_count) + epsilon)
        scaling = cost_diag + penalty + low_dual / dispatch + high_dual / (capacity - dispatch)
        updated = jnp.clip(
            dispatch - step_size * residual / (scaling * (1.0 + dual_rms)), lowest, highest
        )
        low_dual = low_dual + step_size * (target / updated - low_dual)
        high_dual = high_dual + step_size * (target / (capacity - updated) - high_dual)
        prices = prices + step_size * imbalance / (1.0 + primal_rms)
        dispatch = updated
    return (dispatch, prices, plan)


def solution(mesh):
    torus = Mesh(
        mesh.devices.reshape(8, 2, 2, 4, 2), ("scen_0", "scen_1", "gen_0", "gen_1", "gen_2")
    )
    placed = (
        P(SCEN, None, None),
        P(None, GEN),
        P(GEN),
        P(GEN),
        P(GEN, None, None),
        P(SCEN, GEN, None, None),
        P(SCEN, GEN),
        P(GEN),
        P(),
        P(),
    )
    return jax.shard_map(
        local,
        mesh=torus,
        in_specs=placed,
        out_specs=(P(SCEN, None, GEN), P(SCEN, None, None), P(None, GEN)),
        check_vma=False,
    )
```

profile of v0, /device:TPU:1, one launch (start us, length us, event | category | flops | bytes accessed | tf_op | source)
XLA Modules:
  0.0 563.8 jit_solution(9734501786071534831)
XLA Ops:
  11.2 11.8 %all-to-all-start = ((f32[16,16,1280]{2,1,0:T(8,128)}), f32[16,16,1280]{2,1,0:T(8,128)}, u32[]{:S(2)}, u32[]{:S(2)}) async-start(f32[16,16,1280]{2,1,0:T(8,128)} %broadcast_in_dim.30), calls=%async_computation | async-start | bytes 2621440 | tf_op jit(solution)/shard_map/all_to_all | solution.py:19
  30.3 24.3 %all-to-all-done = f32[16,16,1280]{2,1,0:T(8,128)} async-done(((f32[16,16,1280]{2,1,0:T(8,128)}), f32[16,16,1280]{2,1,0:T(8,128)}, u32[]{:S(2)}, u32[]{:S(2)}) %all-to-all-start) | async-done | bytes 1310752 | tf_op jit(solution)/shard_map/all_to_all | solution.py:19
  70.8 14.7 %psum.175 = f32[3]{0:T(128)S(1)} all-reduce(f32[3]{0:T(128)S(1)} %pad_maximum_fusion), channel_id=1, replica_groups=mesh['scen_0'=8,'scen_1'=2,'gen_0'=2,'gen_1'=4,'gen_2'=2] {'scen_0'}, use_global_device_ids=true, to_apply=%region_6.0 | all-reduce | flops 3 | bytes 24 | tf_op jit(solution)/shard_map/psum | solution.py:33
  96.8 7.0 %psum.178 = f32[3]{0:T(128)S(1)} all-reduce(f32[3]{0:T(128)S(1)} %psum.177), channel_id=1, replica_groups=mesh['scen_0'=8,'scen_1'=2,'gen_0'=2,'gen_1'=4,'gen_2'=2] {'gen_1'}, use_global_device_ids=true, to_apply=%region_9.0 | all-reduce | flops 3 | bytes 24 | tf_op jit(solution)/shard_map/psum | solution.py:33
  103.8 10.2 %psum.179 = f32[3]{0:T(128)S(1)} all-reduce(f32[3]{0:T(128)S(1)} %psum.178), channel_id=1, replica_groups=mesh['scen_0'=8,'scen_1'=2,'gen_0'=2,'gen_1'=4,'gen_2'=2] {'gen_2'}, use_global_device_ids=true, to_apply=%region_10.0 | all-reduce | flops 3 | bytes 24 | tf_op jit(solution)/shard_map/psum | solution.py:33
  121.7 6.3 %all-to-all-start.1 = ((f32[16,16,1280]{2,1,0:T(8,128)}), f32[16,16,1280]{2,1,0:T(8,128)}, u32[]{:S(2)}, u32[]{:S(2)}) async-start(f32[16,16,1280]{2,1,0:T(8,128)} %broadcast_in_dim.32), calls=%async_computation.1 | async-start | bytes 2621440 | tf_op jit(solution)/shard_map/all_to_all | solution.py:19
  137.0 22.9 %all-to-all-done.1 = f32[16,16,1280]{2,1,0:T(8,128)} async-done(((f32[16,16,1280]{2,1,0:T(8,128)}), f32[16,16,1280]{2,1,0:T(8,128)}, u32[]{:S(2)}, u32[]{:S(2)}) %all-to-all-start.1) | async-done | bytes 1310752 | tf_op jit(solution)/shard_map/all_to_all | solution.py:19
  172.5 14.5 %psum.180 = f32[3]{0:T(128)S(1)} all-reduce(f32[3]{0:T(128)S(1)} %pad_maximum_fusion.1), channel_id=1, replica_groups=mesh['scen_0'=8,'scen_1'=2,'gen_0'=2,'gen_1'=4,'gen_2'=2] {'scen_0'}, use_global_device_ids=true, to_apply=%region_17.18 | all-reduce | flops 3 | bytes 24 | tf_op jit(solution)/shard_map/psum | solution.py:33
  197.6 6.3 %psum.183 = f32[3]{0:T(128)S(1)} all-reduce(f32[3]{0:T(128)S(1)} %psum.182), channel_id=1, replica_groups=mesh['scen_0'=8,'scen_1'=2,'gen_0'=2,'gen_1'=4,'gen_2'=2] {'gen_1'}, use_global_device_ids=true, to_apply=%region_20.21 | all-reduce | flops 3 | bytes 24 | tf_op jit(solution)/shard_map/psum | solution.py:33
  204.0 10.3 %psum.184 = f32[3]{0:T(128)S(1)} all-reduce(f32[3]{0:T(128)S(1)} %psum.183), channel_id=1, replica_groups=mesh['scen_0'=8,'scen_1'=2,'gen_0'=2,'gen_1'=4,'gen_2'=2] {'gen_2'}, use_global_device_ids=true, to_apply=%region_21.22 | all-reduce | flops 3 | bytes 24 | tf_op jit(solution)/shard_map/psum | solution.py:33
  223.9 6.5 %all-to-all-start.2 = ((f32[16,16,1280]{2,1,0:T(8,128)}), f32[16,16,1280]{2,1,0:T(8,128)}, u32[]{:S(2)}, u32[]{:S(2)}) async-start(f32[16,16,1280]{2,1,0:T(8,128)} %broadcast_in_dim.33), calls=%async_computation.2 | async-start | bytes 2621440 | tf_op jit(solution)/shard_map/all_to_all | solution.py:19
  242.2 20.0 %all-to-all-done.2 = f32[16,16,1280]{2,1,0:T(8,128)} async-done(((f32[16,16,1280]{2,1,0:T(8,128)}), f32[16,16,1280]{2,1,0:T(8,128)}, u32[]{:S(2)}, u32[]{:S(2)}) %all-to-all-start.2) | async-done | bytes 1310752 | tf_op jit(solution)/shard_map/all_to_all | solution.py:19
  282.3 14.8 %psum.185 = f32[3]{0:T(128)S(1)} all-reduce(f32[3]{0:T(128)S(1)} %pad_maximum_fusion.2), channel_id=1, replica_groups=mesh['scen_0'=8,'scen_1'=2,'gen_0'=2,'gen_1'=4,'gen_2'=2] {'scen_0'}, use_global_device_ids=true, to_apply=%region_28.29 | all-reduce | flops 3 | bytes 24 | tf_op jit(solution)/shard_map/psum | solution.py:33
  307.7 6.7 %psum.188 = f32[3]{0:T(128)S(1)} all-reduce(f32[3]{0:T(128)S(1)} %psum.187), channel_id=1, replica_groups=mesh['scen_0'=8,'scen_1'=2,'gen_0'=2,'gen_1'=4,'gen_2'=2] {'gen_1'}, use_global_device_ids=true, to_apply=%region_31.32 | all-reduce | flops 3 | bytes 24 | tf_op jit(solution)/shard_map/psum | solution.py:33
  314.4 10.2 %psum.189 = f32[3]{0:T(128)S(1)} all-reduce(f32[3]{0:T(128)S(1)} %psum.188), channel_id=1, replica_groups=mesh['scen_0'=8,'scen_1'=2,'gen_0'=2,'gen_1'=4,'gen_2'=2] {'gen_2'}, use_global_device_ids=true, to_apply=%region_32.33 | all-reduce | flops 3 | bytes 24 | tf_op jit(solution)/shard_map/psum | solution.py:33
  334.8 6.7 %all-to-all-start.3 = ((f32[16,16,1280]{2,1,0:T(8,128)}), f32[16,16,1280]{2,1,0:T(8,128)}, u32[]{:S(2)}, u32[]{:S(2)}) async-start(f32[16,16,1280]{2,1,0:T(8,128)} %broadcast_in_dim.34), calls=%async_computation.3 | async-start | bytes 2621440 | tf_op jit(solution)/shard_map/all_to_all | solution.py:19
  351.5 21.8 %all-to-all-done.3 = f32[16,16,1280]{2,1,0:T(8,128)} async-done(((f32[16,16,1280]{2,1,0:T(8,128)}), f32[16,16,1280]{2,1,0:T(8,128)}, u32[]{:S(2)}, u32[]{:S(2)}) %all-to-all-start.3) | async-done | bytes 1310752 | tf_op jit(solution)/shard_map/all_to_all | solution.py:19
  388.4 15.2 %psum.190 = f32[3]{0:T(128)} all-reduce(f32[3]{0:T(128)} %pad_maximum_fusion.3), channel_id=1, replica_groups=mesh['scen_0'=8,'scen_1'=2,'gen_0'=2,'gen_1'=4,'gen_2'=2] {'scen_0'}, use_global_device_ids=true, to_apply=%region_39.40 | all-reduce | flops 3 | bytes 24 | tf_op jit(solution)/shard_map/psum | solution.py:33
  415.3 7.4 %psum.193 = f32[3]{0:T(128)} all-reduce(f32[3]{0:T(128)} %psum.192), channel_id=1, replica_groups=mesh['scen_0'=8,'scen_1'=2,'gen_0'=2,'gen_1'=4,'gen_2'=2] {'gen_1'}, use_global_device_ids=true, to_apply=%region_42.43 | all-reduce | flops 3 | bytes 24 | tf_op jit(solution)/shard_map/psum | solution.py:33
  422.7 11.6 %psum.194 = f32[3]{0:T(128)} all-reduce(f32[3]{0:T(128)} %psum.193), channel_id=1, replica_groups=mesh['scen_0'=8,'scen_1'=2,'gen_0'=2,'gen_1'=4,'gen_2'=2] {'gen_2'}, use_global_device_ids=true, to_apply=%region_43.44 | all-reduce | flops 3 | bytes 24 | tf_op jit(solution)/shard_map/psum | solution.py:33
  460.5 22.0 %all-to-all-done.4 = f32[16,16,1280]{2,1,0:T(8,128)} async-done(((f32[16,16,1280]{2,1,0:T(8,128)}), f32[16,16,1280]{2,1,0:T(8,128)}, u32[]{:S(2)}, u32[]{:S(2)}) %all-to-all-start.4) | async-done | bytes 1310752 | tf_op jit(solution)/shard_map/all_to_all | solution.py:19
  503.7 15.5 %psum.195 = f32[3]{0:T(128)} all-reduce(f32[3]{0:T(128)} %pad_maximum_fusion.4), channel_id=1, replica_groups=mesh['scen_0'=8,'scen_1'=2,'gen_0'=2,'gen_1'=4,'gen_2'=2] {'scen_0'}, use_global_device_ids=true, to_apply=%region_50.51 | all-reduce | flops 3 | bytes 24 | tf_op jit(solution)/shard_map/psum | solution.py:33
  530.7 7.0 %psum.198 = f32[3]{0:T(128)} all-reduce(f32[3]{0:T(128)} %psum.197), channel_id=1, replica_groups=mesh['scen_0'=8,'scen_1'=2,'gen_0'=2,'gen_1'=4,'gen_2'=2] {'gen_1'}, use_global_device_ids=true, to_apply=%region_53.54 | all-reduce | flops 3 | bytes 24 | tf_op jit(solution)/shard_map/psum | solution.py:33
  537.7 11.1 %psum.199 = f32[3]{0:T(128)} all-reduce(f32[3]{0:T(128)} %psum.198), channel_id=1, replica_groups=mesh['scen_0'=8,'scen_1'=2,'gen_0'=2,'gen_1'=4,'gen_2'=2] {'gen_2'}, use_global_device_ids=true, to_apply=%region_54.55 | all-reduce | flops 3 | bytes 24 | tf_op jit(solution)/shard_map/psum | solution.py:33
  (192 shorter events, 225.3 us)
Async XLA Ops:
  7.2 16.7 %copy-start = (bf16[5,256,256]{2,1,0:T(8,128)(2,1)S(1)}, bf16[5,256,256]{2,1,0:T(8,128)(2,1)}, u32[]{:S(2)}) copy-start(bf16[5,256,256]{2,1,0:T(8,128)(2,1)} %param.14) | copy-start | bytes 1966084
  7.2 57.8 %all-gather.11.cloned.1.call-start = ((), (), s32[]{:S(2)}) async-start(), calls=%async_computation.5 | async-start | bytes 4456448 | tf_op jit(solution)/shard_map/all_gather | solution.py:27
  11.2 43.4 %all-to-all-start = ((f32[16,16,1280]{2,1,0:T(8,128)}), f32[16,16,1280]{2,1,0:T(8,128)}, u32[]{:S(2)}, u32[]{:S(2)}) async-start(f32[16,16,1280]{2,1,0:T(8,128)} %broadcast_in_dim.30), calls=%async_computation | async-start | bytes 2621440 | tf_op jit(solution)/shard_map/all_to_all | solution.py:19
  23.0 144.4 %all-gather.13.cloned.1.call-start = ((), (), s32[]{:S(2)}) async-start(), calls=%async_computation.6 | async-start | bytes 4456448 | tf_op jit(solution)/shard_map/all_gather | solution.py:27
  29.4 26.7 %copy-start.25 = (f32[16,1280]{1,0:T(8,128)S(1)}, f32[16,1280]{1,0:T(8,128)}, u32[]{:S(2)}) copy-start(f32[16,1280]{1,0:T(8,128)} %param.11) | copy-start | bytes 245764
  30.3 85.6 %copy-start.19 = (f32[1280]{0:T(1024)}, f32[1280]{0:T(1024)S(1)}, u32[]{:S(2)}) copy-start(f32[1280]{0:T(1024)S(1)} %get-tuple-element.24) | copy-start | bytes 15364
  30.3 85.6 %copy-start.20 = (f32[1280]{0:T(1024)}, f32[1280]{0:T(1024)S(1)}, u32[]{:S(2)}) copy-start(f32[1280]{0:T(1024)S(1)} %get-tuple-element.25) | copy-start | bytes 15364
  65.0 5.2 copy-start.32
  65.0 20.5 %copy-start.33 = (s32[5]{0:T(128)S(1)}, s32[5]{0:T(128)}, u32[]{:S(2)}) copy-start(s32[5]{0:T(128)} %param.19) | copy-start | bytes 64
  67.5 48.4 %copy-start.13 = (f32[256,256]{1,0:T(8,128)}, f32[256,256]{1,0:T(8,128)S(1)}, u32[]{:S(2)}) copy-start(f32[256,256]{1,0:T(8,128)S(1)} %reduce_sum.274) | copy-start | bytes 786436
  67.5 48.4 %copy-start.15 = (f32[256,256]{1,0:T(8,128)}, f32[256,256]{1,0:T(8,128)S(1)}, u32[]{:S(2)}) copy-start(f32[256,256]{1,0:T(8,128)S(1)} %broadcast_multiply_fusion.4) | copy-start | bytes 786436
  121.7 38.1 %all-to-all-start.1 = ((f32[16,16,1280]{2,1,0:T(8,128)}), f32[16,16,1280]{2,1,0:T(8,128)}, u32[]{:S(2)}, u32[]{:S(2)}) async-start(f32[16,16,1280]{2,1,0:T(8,128)} %broadcast_in_dim.32), calls=%async_computation.1 | async-start | bytes 2621440 | tf_op jit(solution)/shard_map/all_to_all | solution.py:19
  128.1 140.4 %all-gather.15.cloned.1.call-start = ((), (), s32[]{:S(2)}) async-start(), calls=%async_computation.7 | async-start | bytes 4456448 | tf_op jit(solution)/shard_map/all_gather | solution.py:27
  169.9 46.4 %copy-start.14 = (f32[256,256]{1,0:T(8,128)}, f32[256,256]{1,0:T(8,128)S(1)}, u32[]{:S(2)}) copy-start(f32[256,256]{1,0:T(8,128)S(1)} %reduce_sum.280) | copy-start | bytes 786436
  220.2 55.6 %copy-start.1 = (f32[16,16,1280]{2,1,0:T(8,128)}, f32[16,16,1280]{2,1,0:T(8,128)S(1)}, u32[]{:S(2)}) copy-start(f32[16,16,1280]{2,1,0:T(8,128)S(1)} %get-tuple-element.15) | copy-start | bytes 3932164
  223.9 38.3 %all-to-all-start.2 = ((f32[16,16,1280]{2,1,0:T(8,128)}), f32[16,16,1280]{2,1,0:T(8,128)}, u32[]{:S(2)}, u32[]{:S(2)}) async-start(f32[16,16,1280]{2,1,0:T(8,128)} %broadcast_in_dim.33), calls=%async_computation.2 | async-start | bytes 2621440 | tf_op jit(solution)/shard_map/all_to_all | solution.py:19
  230.5 150.5 %all-gather.17.cloned.1.call-start = ((), (), s32[]{:S(2)}) async-start(), calls=%async_computation.8 | async-start | bytes 4456448 | tf_op jit(solution)/shard_map/all_gather | solution.py:27
  326.6 5.3 copy-start.23
  334.8 38.5 %all-to-all-start.3 = ((f32[16,16,1280]{2,1,0:T(8,128)}), f32[16,16,1280]{2,1,0:T(8,128)}, u32[]{:S(2)}, u32[]{:S(2)}) async-start(f32[16,16,1280]{2,1,0:T(8,128)} %broadcast_in_dim.34), calls=%async_computation.3 | async-start | bytes 2621440 | tf_op jit(solution)/shard_map/all_to_all | solution.py:19
  341.5 147.8 %all-gather.19.cloned.1.call-start = ((), (), s32[]{:S(2)}) async-start(), calls=%async_computation.9 | async-start | bytes 4456448 | tf_op jit(solution)/shard_map/all_gather | solution.py:27
  351.5 24.8 %copy-start.2 = (f32[16,16,1280]{2,1,0:T(8,128)S(1)}, f32[16,16,1280]{2,1,0:T(8,128)}, u32[]{:S(2)}) copy-start(f32[16,16,1280]{2,1,0:T(8,128)} %get-tuple-element.12) | copy-start | bytes 3932164
  437.0 4.9 copy-start.24
  444.7 6.0 %copy-start.5 = (f32[16,16,1280]{2,1,0:T(8,128)S(1)}, f32[16,16,1280]{2,1,0:T(8,128)}, u32[]{:S(2)}) copy-start(f32[16,16,1280]{2,1,0:T(8,128)} %copy-done.4) | copy-start | bytes 3932164
  444.7 37.7 %all-to-all-start.4 = ((f32[16,16,1280]{2,1,0:T(8,128)}), f32[16,16,1280]{2,1,0:T(8,128)}, u32[]{:S(2)}, u32[]{:S(2)}) async-start(f32[16,16,1280]{2,1,0:T(8,128)} %broadcast_in_dim.35), calls=%async_computation.4 | async-start | bytes 2621440 | tf_op jit(solution)/shard_map/all_to_all | solution.py:19
  (21 other events, 38.3 us)
Sparse Core Ops, SparseCore 0:
  10.4 54.4 all-gather.10
  120.7 46.2 all-gather.12
  222.0 46.4 all-gather.14
  333.7 46.8 all-gather.16
  443.7 45.6 all-gather.18
where the time goes:
time: 573 us; the launch traced here: 564 us
  blocking collectives  211 us (37%)
  waiting for transfers between devices  125 us (22%)
  other arithmetic  71.2 us (12%)
  local copies, waits for them, and re-layouts  47.5 us (8%)
  starting transfers between devices  38.5 us (7%)
  matrix products  36.9 us (6%)
  between operations  33.8 us (6%)
    psum x25, blocking collectives, by_axis(): value = lax.psum(value, axis)  211 us
    all_to_all x5, waiting for transfers between devices, copy_for_each(): return lax.all_to_all(copies, axis, split_axis=0, concat_axis=0, tiled=True)  111 us
    all_to_all x5, starting transfers between devices, copy_for_each(): return lax.all_to_all(copies, axis, split_axis=0, concat_axis=0, tiled=True)  37.3 us
    dot_general x5, matrix products, local(): jnp.dot(prices.reshape(row_count, zone_count), onehot.T, precision=lax.Pr...  22.2 us
    reduce_sum x5, other arithmetic, local(): gap_local = jnp.sum(dispatch * low_dual + (capacity - dispatch) * high_dual)  16.9 us
    reduce_sum x5, other arithmetic, over_pieces(): return blocks.sum(axis=0)  14.5 us
    all_gather x5, waiting for transfers between devices, over_pieces(): blocks = lax.all_gather(value, axis)  13.8 us
    reshape x5, local copies, waits for them, and re-layouts, local(): (own_part + cross_part * block_mask[None, :, None]).reshape(local_scen, p...  12.1 us
  transfers between devices with their start and end apart: 10, of which 8 were waited for; matrix products, arithmetic and copies ran while one was open for 13% of the time, Pallas kernels for 0%

commit v1 on v0

--- a/solution.py
+++ b/solution.py
@@ -12,6 +12,12 @@
 penalty = 2.0
 centering = 0.5
 epsilon = 1e-06
+
+
+def summed_here(x, mesh_axis):
+    blocks = lax.all_gather(x, mesh_axis, axis=0, tiled=False)
+    result = blocks.sum(axis=0)
+    return result
 
 
 def copy_for_each(value, axis):
@@ -30,7 +36,7 @@
 
 def by_axis(value, axes):
     for axis in axes:
-        value = lax.psum(value, axis)
+        value = summed_here(value, axis)
     return value
 
 

time: 573 us -> 620 us (1.082)
  local copies, waits for them, and re-layouts: 47.5 us -> 82.3 us
  other arithmetic: 71.2 us -> 85.3 us
  waiting for transfers between devices: 125 us -> 118 us
    psum x25 -> x0, blocking collectives: 211 us -> none  [by_axis(): value = lax.psum(value, axis)]
    unnamed x0 -> x25, blocking collectives: none -> 211 us
    unnamed x70 -> x130, local copies, waits for them, and re-layouts: 3.36 us -> 24.4 us
    all_gather x0 -> x25, local copies, waits for them, and re-layouts: none -> 13.9 us  [summed_here(): blocks = lax.all_gather(x, mesh_axis, axis=0, tiled=False)]
    reduce_sum x0 -> x25, other arithmetic: none -> 12.4 us  [summed_here(): result = blocks.sum(axis=0)]
    unnamed x0 -> x5, other arithmetic: none -> 9.17 us
    another operation x5 -> x0, other arithmetic: 7.5 us -> none  [local(): stacked = jnp.stack([gap_local, dual_local, primal_local])]
    all_to_all x5, waiting for transfers between devices: 111 us -> 104 us  [copy_for_each(): return lax.all_to_all(copies, axis, split_axis=0, concat_axis=0, tiled=True)]
where the time goes in v1:
time: 620 us; the launch traced here: 609 us
  blocking collectives  211 us (34%)
  waiting for transfers between devices  118 us (19%)
  other arithmetic  85.3 us (14%)
  local copies, waits for them, and re-layouts  82.3 us (13%)
  starting transfers between devices  38.5 us (6%)
  between operations  37.3 us (6%)
  matrix products  36.9 us (6%)
    unnamed x25, blocking collectives  211 us
    all_to_all x5, waiting for transfers between devices, copy_for_each(): return lax.all_to_all(copies, axis, split_axis=0, concat_axis=0, tiled=True)  104 us
    all_to_all x5, starting transfers between devices, copy_for_each(): return lax.all_to_all(copies, axis, split_axis=0, concat_axis=0, tiled=True)  37.6 us
    unnamed x130, local copies, waits for them, and re-layouts  24.4 us
    dot_general x5, matrix products, local(): jnp.dot(prices.reshape(row_count, zone_count), onehot.T, precision=lax.Pr...  22.2 us
    reduce_sum x5, other arithmetic, local(): gap_local = jnp.sum(dispatch * low_dual + (capacity - dispatch) * high_dual)  16.9 us
    reduce_sum x5, other arithmetic, over_pieces(): return blocks.sum(axis=0)  14.5 us
    all_gather x25, local copies, waits for them, and re-layouts, summed_here(): blocks = lax.all_gather(x, mesh_axis, axis=0, tiled=False)  13.9 us
  transfers between devices with their start and end apart: 10, of which 8 were waited for; matrix products, arithmetic and copies ran while one was open for 13% of the time, Pallas kernels for 0%

profile of v1, /device:TPU:1, one launch (start us, length us, event | category | flops | bytes accessed | tf_op | source)
XLA Modules:
  0.0 609.3 jit_solution(71296454570223554)
XLA Ops:
  11.2 11.8 %all-to-all-start = ((f32[16,16,1280]{2,1,0:T(8,128)}), f32[16,16,1280]{2,1,0:T(8,128)}, u32[]{:S(2)}, u32[]{:S(2)}) async-start(f32[16,16,1280]{2,1,0:T(8,128)} %broadcast_in_dim.30), calls=%async_computation | async-start | bytes 2621440 | tf_op jit(solution)/shard_map/all_to_all | solution.py:25
  37.4 17.2 %all-to-all-done = f32[16,16,1280]{2,1,0:T(8,128)} async-done(((f32[16,16,1280]{2,1,0:T(8,128)}), f32[16,16,1280]{2,1,0:T(8,128)}, u32[]{:S(2)}, u32[]{:S(2)}) %all-to-all-start) | async-done | bytes 1310752 | tf_op jit(solution)/shard_map/all_to_all | solution.py:25
  70.1 14.7 %all-reduce = f32[24]{0:T(128)S(1)} all-reduce(f32[24]{0:T(128)S(1)} %maximum_dynamic-update-slice_fusion), channel_id=3, replica_groups=mesh['scen_0'=8,'scen_1'=2,'gen_0'=2,'gen_1'=4,'gen_2'=2] {'scen_0'}, use_global_device_ids=true, to_apply=%add | all-reduce | flops 24 | bytes 192
  96.9 6.9 %all-reduce.3 = f32[12]{0:T(128)S(1)} all-reduce(f32[12]{0:T(128)S(1)} %dynamic-update-slice.3), channel_id=6, replica_groups=mesh['scen_0'=8,'scen_1'=2,'gen_0'=2,'gen_1'=4,'gen_2'=2] {'gen_1'}, use_global_device_ids=true, to_apply=%add.3 | all-reduce | flops 12 | bytes 96
  104.3 10.4 %all-reduce.4 = f32[6]{0:T(128)S(1)} all-reduce(f32[6]{0:T(128)S(1)} %dynamic-update-slice.4), channel_id=7, replica_groups=mesh['scen_0'=8,'scen_1'=2,'gen_0'=2,'gen_1'=4,'gen_2'=2] {'gen_2'}, use_global_device_ids=true, to_apply=%add.4 | all-reduce | flops 6 | bytes 48
  122.4 6.5 %all-to-all-start.1 = ((f32[16,16,1280]{2,1,0:T(8,128)}), f32[16,16,1280]{2,1,0:T(8,128)}, u32[]{:S(2)}, u32[]{:S(2)}) async-start(f32[16,16,1280]{2,1,0:T(8,128)} %broadcast_in_dim.32), calls=%async_computation.1 | async-start | bytes 2621440 | tf_op jit(solution)/shard_map/all_to_all | solution.py:25
  137.7 23.0 %all-to-all-done.1 = f32[16,16,1280]{2,1,0:T(8,128)} async-done(((f32[16,16,1280]{2,1,0:T(8,128)}), f32[16,16,1280]{2,1,0:T(8,128)}, u32[]{:S(2)}, u32[]{:S(2)}) %all-to-all-start.1) | async-done | bytes 1310752 | tf_op jit(solution)/shard_map/all_to_all | solution.py:25
  173.4 14.5 %all-reduce.5 = f32[24]{0:T(128)S(1)} all-reduce(f32[24]{0:T(128)S(1)} %maximum_dynamic-update-slice_fusion.1), channel_id=9, replica_groups=mesh['scen_0'=8,'scen_1'=2,'gen_0'=2,'gen_1'=4,'gen_2'=2] {'scen_0'}, use_global_device_ids=true, to_apply=%add.5 | all-reduce | flops 24 | bytes 192
  199.6 6.3 %all-reduce.8 = f32[12]{0:T(128)S(1)} all-reduce(f32[12]{0:T(128)S(1)} %dynamic-update-slice.8), channel_id=12, replica_groups=mesh['scen_0'=8,'scen_1'=2,'gen_0'=2,'gen_1'=4,'gen_2'=2] {'gen_1'}, use_global_device_ids=true, to_apply=%add.8 | all-reduce | flops 12 | bytes 96
  206.3 10.2 %all-reduce.9 = f32[6]{0:T(128)S(1)} all-reduce(f32[6]{0:T(128)S(1)} %dynamic-update-slice.9), channel_id=13, replica_groups=mesh['scen_0'=8,'scen_1'=2,'gen_0'=2,'gen_1'=4,'gen_2'=2] {'gen_2'}, use_global_device_ids=true, to_apply=%add.9 | all-reduce | flops 6 | bytes 48
  226.2 6.6 %all-to-all-start.2 = ((f32[16,16,1280]{2,1,0:T(8,128)}), f32[16,16,1280]{2,1,0:T(8,128)}, u32[]{:S(2)}, u32[]{:S(2)}) async-start(f32[16,16,1280]{2,1,0:T(8,128)} %broadcast_in_dim.33), calls=%async_computation.2 | async-start | bytes 2621440 | tf_op jit(solution)/shard_map/all_to_all | solution.py:25
  244.2 20.4 %all-to-all-done.2 = f32[16,16,1280]{2,1,0:T(8,128)} async-done(((f32[16,16,1280]{2,1,0:T(8,128)}), f32[16,16,1280]{2,1,0:T(8,128)}, u32[]{:S(2)}, u32[]{:S(2)}) %all-to-all-start.2) | async-done | bytes 1310752 | tf_op jit(solution)/shard_map/all_to_all | solution.py:25
  285.0 14.6 %all-reduce.10 = f32[24]{0:T(128)S(1)} all-reduce(f32[24]{0:T(128)S(1)} %maximum_dynamic-update-slice_fusion.2), channel_id=15, replica_groups=mesh['scen_0'=8,'scen_1'=2,'gen_0'=2,'gen_1'=4,'gen_2'=2] {'scen_0'}, use_global_device_ids=true, to_apply=%add.10 | all-reduce | flops 24 | bytes 192
  311.1 6.6 %all-reduce.13 = f32[12]{0:T(128)S(1)} all-reduce(f32[12]{0:T(128)S(1)} %dynamic-update-slice.13), channel_id=18, replica_groups=mesh['scen_0'=8,'scen_1'=2,'gen_0'=2,'gen_1'=4,'gen_2'=2] {'gen_1'}, use_global_device_ids=true, to_apply=%add.13 | all-reduce | flops 12 | bytes 96
  318.1 10.5 %all-reduce.14 = f32[6]{0:T(128)S(1)} all-reduce(f32[6]{0:T(128)S(1)} %dynamic-update-slice.14), channel_id=19, replica_groups=mesh['scen_0'=8,'scen_1'=2,'gen_0'=2,'gen_1'=4,'gen_2'=2] {'gen_2'}, use_global_device_ids=true, to_apply=%add.14 | all-reduce | flops 6 | bytes 48
  339.0 6.7 %all-to-all-start.3 = ((f32[16,16,1280]{2,1,0:T(8,128)}), f32[16,16,1280]{2,1,0:T(8,128)}, u32[]{:S(2)}, u32[]{:S(2)}) async-start(f32[16,16,1280]{2,1,0:T(8,128)} %broadcast_in_dim.34), calls=%async_computation.3 | async-start | bytes 2621440 | tf_op jit(solution)/shard_map/all_to_all | solution.py:25
  355.7 21.7 %all-to-all-done.3 = f32[16,16,1280]{2,1,0:T(8,128)} async-done(((f32[16,16,1280]{2,1,0:T(8,128)}), f32[16,16,1280]{2,1,0:T(8,128)}, u32[]{:S(2)}, u32[]{:S(2)}) %all-to-all-start.3) | async-done | bytes 1310752 | tf_op jit(solution)/shard_map/all_to_all | solution.py:25
  393.7 15.2 %all-reduce.15 = f32[24]{0:T(128)} all-reduce(f32[24]{0:T(128)} %maximum_dynamic-update-slice_fusion.3), channel_id=21, replica_groups=mesh['scen_0'=8,'scen_1'=2,'gen_0'=2,'gen_1'=4,'gen_2'=2] {'scen_0'}, use_global_device_ids=true, to_apply=%add.15 | all-reduce | flops 24 | bytes 192
  433.5 7.2 %all-reduce.18 = f32[12]{0:T(128)} all-reduce(f32[12]{0:T(128)} %dynamic-update-slice.18), channel_id=24, replica_groups=mesh['scen_0'=8,'scen_1'=2,'gen_0'=2,'gen_1'=4,'gen_2'=2] {'gen_1'}, use_global_device_ids=true, to_apply=%add.18 | all-reduce | flops 12 | bytes 96
  445.0 11.9 %all-reduce.19 = f32[6]{0:T(128)} all-reduce(f32[6]{0:T(128)} %dynamic-update-slice.19), channel_id=25, replica_groups=mesh['scen_0'=8,'scen_1'=2,'gen_0'=2,'gen_1'=4,'gen_2'=2] {'gen_2'}, use_global_device_ids=true, to_apply=%add.19 | all-reduce | flops 6 | bytes 48
  485.6 22.0 %all-to-all-done.4 = f32[16,16,1280]{2,1,0:T(8,128)} async-done(((f32[16,16,1280]{2,1,0:T(8,128)}), f32[16,16,1280]{2,1,0:T(8,128)}, u32[]{:S(2)}, u32[]{:S(2)}) %all-to-all-start.4) | async-done | bytes 1310752 | tf_op jit(solution)/shard_map/all_to_all | solution.py:25
  529.8 15.2 %all-reduce.20 = f32[24]{0:T(128)} all-reduce(f32[24]{0:T(128)} %maximum_dynamic-update-slice_fusion.4), channel_id=27, replica_groups=mesh['scen_0'=8,'scen_1'=2,'gen_0'=2,'gen_1'=4,'gen_2'=2] {'scen_0'}, use_global_device_ids=true, to_apply=%add.20 | all-reduce | flops 24 | bytes 192
  569.3 7.4 %all-reduce.23 = f32[12]{0:T(128)} all-reduce(f32[12]{0:T(128)} %dynamic-update-slice.23), channel_id=30, replica_groups=mesh['scen_0'=8,'scen_1'=2,'gen_0'=2,'gen_1'=4,'gen_2'=2] {'gen_1'}, use_global_device_ids=true, to_apply=%add.23 | all-reduce | flops 12 | bytes 96
  580.9 10.8 %all-reduce.24 = f32[6]{0:T(128)} all-reduce(f32[6]{0:T(128)} %dynamic-update-slice.24), channel_id=31, replica_groups=mesh['scen_0'=8,'scen_1'=2,'gen_0'=2,'gen_1'=4,'gen_2'=2] {'gen_2'}, use_global_device_ids=true, to_apply=%add.24 | all-reduce | flops 6 | bytes 48
  (302 shorter events, 273.5 us)
Async XLA Ops:
  7.2 16.7 %copy-start = (bf16[5,256,256]{2,1,0:T(8,128)(2,1)S(1)}, bf16[5,256,256]{2,1,0:T(8,128)(2,1)}, u32[]{:S(2)}) copy-start(bf16[5,256,256]{2,1,0:T(8,128)(2,1)} %param.14) | copy-start | bytes 1966084
  7.2 57.7 %all-gather.36.cloned.1.call-start = ((), (), s32[]{:S(2)}) async-start(), calls=%async_computation.5 | async-start | bytes 4456448 | tf_op jit(solution)/shard_map/all_gather | solution.py:33
  11.2 43.4 %all-to-all-start = ((f32[16,16,1280]{2,1,0:T(8,128)}), f32[16,16,1280]{2,1,0:T(8,128)}, u32[]{:S(2)}, u32[]{:S(2)}) async-start(f32[16,16,1280]{2,1,0:T(8,128)} %broadcast_in_dim.30), calls=%async_computation | async-start | bytes 2621440 | tf_op jit(solution)/shard_map/all_to_all | solution.py:25
  23.0 145.2 %all-gather.38.cloned.1.call-start = ((), (), s32[]{:S(2)}) async-start(), calls=%async_computation.6 | async-start | bytes 4456448 | tf_op jit(solution)/shard_map/all_gather | solution.py:33
  27.5 7.0 %copy-start.35 = (u32[256]{0:T(256)S(1)}, u32[256]{0:T(256)}, u32[]{:S(2)}) copy-start(u32[256]{0:T(256)} %constant.146) | copy-start | bytes 3076
  27.5 7.6 %copy-start.32 = (s32[5]{0:T(128)S(1)}, s32[5]{0:T(128)}, u32[]{:S(2)}) copy-start(s32[5]{0:T(128)} %param.18) | copy-start | bytes 64
  27.5 8.3 %copy-start.33 = (s32[5]{0:T(128)S(1)}, s32[5]{0:T(128)}, u32[]{:S(2)}) copy-start(s32[5]{0:T(128)} %param.19) | copy-start | bytes 64
  27.5 9.9 %copy-start.26 = (f32[1280]{0:T(1024)S(1)}, f32[1280]{0:T(1024)}, u32[]{:S(2)}) copy-start(f32[1280]{0:T(1024)} %param.12) | copy-start | bytes 15364
  29.5 26.5 %copy-start.25 = (f32[16,1280]{1,0:T(8,128)S(1)}, f32[16,1280]{1,0:T(8,128)}, u32[]{:S(2)}) copy-start(f32[16,1280]{1,0:T(8,128)} %param.11) | copy-start | bytes 245764
  37.4 79.2 %copy-start.19 = (f32[1280]{0:T(1024)}, f32[1280]{0:T(1024)S(1)}, u32[]{:S(2)}) copy-start(f32[1280]{0:T(1024)S(1)} %get-tuple-element.24) | copy-start | bytes 15364
  37.4 79.2 %copy-start.20 = (f32[1280]{0:T(1024)}, f32[1280]{0:T(1024)S(1)}, u32[]{:S(2)}) copy-start(f32[1280]{0:T(1024)S(1)} %get-tuple-element.25) | copy-start | bytes 15364
  67.4 49.2 %copy-start.13 = (f32[256,256]{1,0:T(8,128)}, f32[256,256]{1,0:T(8,128)S(1)}, u32[]{:S(2)}) copy-start(f32[256,256]{1,0:T(8,128)S(1)} %reduce_sum.499) | copy-start | bytes 786436
  67.4 49.2 %copy-start.15 = (f32[256,256]{1,0:T(8,128)}, f32[256,256]{1,0:T(8,128)S(1)}, u32[]{:S(2)}) copy-start(f32[256,256]{1,0:T(8,128)S(1)} %broadcast_multiply_fusion.4) | copy-start | bytes 786436
  122.4 38.3 %all-to-all-start.1 = ((f32[16,16,1280]{2,1,0:T(8,128)}), f32[16,16,1280]{2,1,0:T(8,128)}, u32[]{:S(2)}, u32[]{:S(2)}) async-start(f32[16,16,1280]{2,1,0:T(8,128)} %broadcast_in_dim.32), calls=%async_computation.1 | async-start | bytes 2621440 | tf_op jit(solution)/shard_map/all_to_all | solution.py:25
  129.0 142.1 %all-gather.40.cloned.1.call-start = ((), (), s32[]{:S(2)}) async-start(), calls=%async_computation.7 | async-start | bytes 4456448 | tf_op jit(solution)/shard_map/all_gather | solution.py:33
  170.7 47.9 %copy-start.14 = (f32[256,256]{1,0:T(8,128)}, f32[256,256]{1,0:T(8,128)S(1)}, u32[]{:S(2)}) copy-start(f32[256,256]{1,0:T(8,128)S(1)} %reduce_sum.510) | copy-start | bytes 786436
  222.4 55.9 %copy-start.1 = (f32[16,16,1280]{2,1,0:T(8,128)}, f32[16,16,1280]{2,1,0:T(8,128)S(1)}, u32[]{:S(2)}) copy-start(f32[16,16,1280]{2,1,0:T(8,128)S(1)} %get-tuple-element.15) | copy-start | bytes 3932164
  226.2 38.4 %all-to-all-start.2 = ((f32[16,16,1280]{2,1,0:T(8,128)}), f32[16,16,1280]{2,1,0:T(8,128)}, u32[]{:S(2)}, u32[]{:S(2)}) async-start(f32[16,16,1280]{2,1,0:T(8,128)} %broadcast_in_dim.33), calls=%async_computation.2 | async-start | bytes 2621440 | tf_op jit(solution)/shard_map/all_to_all | solution.py:25
  232.8 152.3 %all-gather.42.cloned.1.call-start = ((), (), s32[]{:S(2)}) async-start(), calls=%async_computation.8 | async-start | bytes 4456448 | tf_op jit(solution)/shard_map/all_gather | solution.py:33
  339.0 38.5 %all-to-all-start.3 = ((f32[16,16,1280]{2,1,0:T(8,128)}), f32[16,16,1280]{2,1,0:T(8,128)}, u32[]{:S(2)}, u32[]{:S(2)}) async-start(f32[16,16,1280]{2,1,0:T(8,128)} %broadcast_in_dim.34), calls=%async_computation.3 | async-start | bytes 2621440 | tf_op jit(solution)/shard_map/all_to_all | solution.py:25
  345.6 168.8 %all-gather.44.cloned.1.call-start = ((), (), s32[]{:S(2)}) async-start(), calls=%async_computation.9 | async-start | bytes 4456448 | tf_op jit(solution)/shard_map/all_gather | solution.py:33
  355.7 24.6 %copy-start.2 = (f32[16,16,1280]{2,1,0:T(8,128)S(1)}, f32[16,16,1280]{2,1,0:T(8,128)}, u32[]{:S(2)}) copy-start(f32[16,16,1280]{2,1,0:T(8,128)} %get-tuple-element.12) | copy-start | bytes 3932164
  469.8 6.1 copy-start.5
  469.8 37.8 %all-to-all-start.4 = ((f32[16,16,1280]{2,1,0:T(8,128)}), f32[16,16,1280]{2,1,0:T(8,128)}, u32[]{:S(2)}, u32[]{:S(2)}) async-start(f32[16,16,1280]{2,1,0:T(8,128)} %broadcast_in_dim.35), calls=%async_computation.4 | async-start | bytes 2621440 | tf_op jit(solution)/shard_map/all_to_all | solution.py:25
  (26 other events, 60.8 us)
Sparse Core Ops, SparseCore 0:
  10.4 54.4 all-gather.35
  121.4 46.3 all-gather.37
  224.2 46.7 all-gather.39
  337.9 46.8 all-gather.41
  468.7 45.6 all-gather.43
